TPU v7x, 32 devices: a whole 2x2x4 slice. The times are simulated.
32 devices in a mesh: pr: 4 (over y, x), pc: 8 (over z, core).
Axes of the slice: x: 2, y: 2, z: 4, core: 2. Of those that a mesh axis runs over, the one named last changes fastest.
Arguments:
- pair_state: bfloat16 [96, 96, 128], P('pr', 'pc'), may hold values from -6 to 6
- left_weight: bfloat16 [128, 128], replicated, may hold values from -0.5 to 0.5
- right_weight: bfloat16 [128, 128], replicated, may hold values from -0.5 to 0.5
- mid_gain: float32 [128], replicated, may hold values from 0.25 to 1.75
- out_weight: bfloat16 [128, 128], replicated, may hold values from -0.5 to 0.5
- out_gate: bfloat16 [128, 128], replicated, may hold values from -0.5 to 0.5
Outputs:
- pair_update: bfloat16 [96, 96, 128], P('pr', 'pc')
All inputs are finite; a program needn't handle non-finite values.
Results may differ from a plain program's by a relative error of at most 0.012.
Values may be sent and summed in bfloat16 or wider, within the bound.
A program may use at most 128 MiB of HBM per device.

v0:
```python
import jax
import jax.numpy as jnp
from jax import lax
from jax.sharding import PartitionSpec as P


def scale_channels(values, channel_gain):
    centred = values - jnp.mean(values, axis=-1, keepdims=True)
    return (
        centred
        * lax.rsqrt(jnp.mean(centred * centred, axis=-1, keepdims=True) + 1e-05)
        * channel_gain
    )


def project_pair(pair_in, left_weight, right_weight):
    left = jnp.einsum("ijc,cd->ijd", pair_in, left_weight, preferred_element_type=jnp.float32)
    right = jnp.einsum("ijc,cd->ijd", pair_in, right_weight, preferred_element_type=jnp.float32)
    return (pair_in, left.astype(jnp.bfloat16), right.astype(jnp.bfloat16))


def close_update(mixed, ready, mid_gain, out_weight, out_gate):
    scaled = scale_channels(mixed.astype(jnp.float32), mid_gain).astype(jnp.bfloat16)
    scaled = lax.optimization_barrier(scaled)
    gate = jax.nn.sigmoid(
        jnp.einsum("ijc,cd->ijd", ready, out_gate, preferred_element_type=jnp.float32)
    )
    return (
        jnp.einsum("ijd,dc->ijc", scaled, out_weight, preferred_element_type=jnp.float32) * gate
    ).astype(jnp.bfloat16)


def body(pair_state, left_weight, right_weight, mid_gain, out_weight, out_gate):
    ready, left, right = project_pair(pair_state, left_weight, right_weight)
    count = pair_state.shape[0] * lax.axis_size("pr")
    left_lines, right_lines = (
        lax.all_to_all(left, "pr", split_axis=2, concat_axis=0, tiled=True),
        lax.all_to_all(right, "pr", split_axis=2, concat_axis=0, tiled=True),
    )
    strip = jnp.einsum(
        "kid,kjd->ijd",
        lax.all_gather(left_lines, "pc", axis=1, tiled=True),
        right_lines,
        preferred_element_type=jnp.float32,
    )
    strip = (strip * count ** (-0.5)).astype(jnp.bfloat16)
    mixed = lax.all_to_all(strip, "pr", split_axis=0, concat_axis=2, tiled=True)
    return close_update(mixed, ready, mid_gain, out_weight, out_gate)


def solution(mesh):
    placed = (P("pr", "pc", None), P(), P(), P(), P(), P())
    return jax.shard_map(
        body, mesh=mesh, in_specs=placed, out_specs=P("pr", "pc", None), check_vma=False
    )
```

profile of v0, /device:TPU:0, one launch (start us, length us, event | category | flops | bytes accessed | tf_op | source)
XLA Modules:
  0.0 52.5 jit_solution(6551884356601724737)
XLA Ops:
  0.0 0.0 copy-start
  0.0 0.9 %copy-done = bf16[24,12,128]{2,0,1:T(8,128)(2,1)S(1)} copy-done((bf16[24,12,128]{2,0,1:T(8,128)(2,1)S(1)}, bf16[24,12,128]{2,0,1:T(8,128)(2,1)}, u32[]{:S(2)}) %copy-start) | copy-done | bytes 73752
  0.9 0.9 %convolution_convert_fusion.1 = bf16[24,12,128]{2,0,1:T(8,128)(2,1)S(1)} fusion(bf16[24,12,128]{2,0,1:T(8,128)(2,1)S(1)} %copy-done, bf16[128,128]{1,0:T(8,128)(2,1)} %param.8), kind=kOutput, calls=%fused_computation.10 | convolution fusion | flops 9474048 | bytes 180224 | tf_op jit(solution)/shard_map/ijc,cd->ijd/dot_general | solution.py:18
  1.8 0.4 copy.39
  2.3 1.1 %reshape.28 = bf16[4,2,4608]{2,1,0:T(2,128)(2,1)} reshape(bf16[128,12,24]{2,1,0:T(8,128)(2,1)S(1)} %bitcast.44) | data formatting | bytes 147456
  3.4 0.0 copy-start.1
  3.4 5.3 %all-to-all-start = ((bf16[4,2,4608]{2,1,0:T(2,128)(2,1)}), bf16[4,2,4608]{2,1,0:T(2,128)(2,1)S(1)}, u32[]{:S(2)}, u32[]{:S(2)}) async-start(bf16[4,2,4608]{2,1,0:T(2,128)(2,1)} %reshape.28), calls=%async_computation | async-start | bytes 147456 | tf_op jit(solution)/shard_map/all_to_all | solution.py:38
  8.7 0.0 copy-done.1
  8.7 0.2 convolution_convert_fusion
  8.9 0.4 copy.41
  9.3 1.1 %reshape.26 = bf16[4,2,4608]{2,1,0:T(2,128)(2,1)} reshape(bf16[128,12,24]{2,1,0:T(8,128)(2,1)S(1)} %bitcast.45) | data formatting | bytes 147456
  10.5 3.1 %all-to-all-done = bf16[4,2,4608]{2,1,0:T(2,128)(2,1)S(1)} async-done(((bf16[4,2,4608]{2,1,0:T(2,128)(2,1)}), bf16[4,2,4608]{2,1,0:T(2,128)(2,1)S(1)}, u32[]{:S(2)}, u32[]{:S(2)}) %all-to-all-start) | async-done | bytes 73760 | tf_op jit(solution)/shard_map/all_to_all | solution.py:38
  13.6 3.3 %all-to-all-start.1 = ((bf16[4,2,4608]{2,1,0:T(2,128)(2,1)}), bf16[4,2,4608]{2,1,0:T(2,128)(2,1)S(1)}, u32[]{:S(2)}, u32[]{:S(2)}) async-start(bf16[4,2,4608]{2,1,0:T(2,128)(2,1)} %reshape.26), calls=%async_computation.1 | async-start | bytes 147456 | tf_op jit(solution)/shard_map/all_to_all | solution.py:37
  16.9 0.6 %reshape.29 = bf16[128,12,24]{2,1,0:T(8,128)(2,1)S(1)} reshape(bf16[4,2,4608]{2,1,0:T(2,128)(2,1)S(1)} %all-to-all-done) | data formatting | bytes 147456
  17.5 0.3 copy.55
  17.8 0.2 all_to_all.36
  18.0 3.7 %all-to-all-done.1 = bf16[4,2,4608]{2,1,0:T(2,128)(2,1)S(1)} async-done(((bf16[4,2,4608]{2,1,0:T(2,128)(2,1)}), bf16[4,2,4608]{2,1,0:T(2,128)(2,1)S(1)}, u32[]{:S(2)}, u32[]{:S(2)}) %all-to-all-start.1) | async-done | bytes 73760 | tf_op jit(solution)/shard_map/all_to_all | solution.py:37
  21.7 0.6 %reshape.27 = bf16[128,12,24]{2,1,0:T(8,128)(2,1)S(1)} reshape(bf16[4,2,4608]{2,1,0:T(2,128)(2,1)S(1)} %all-to-all-done.1) | data formatting | bytes 147456
  22.3 0.3 copy.54
  22.6 0.2 all_to_all.40
  22.9 16.5 %all_gather.3 = bf16[96,96,32]{0,2,1:T(8,128)(2,1)S(1)} all-gather(bf16[96,12,32]{0,2,1:T(8,128)(2,1)S(1)} %all_to_all.40), channel_id=1, replica_groups=mesh['pr'=4,'pc'=8] {'pc'}, dimensions={1}, use_global_device_ids=true | all-gather | bytes 663552 | tf_op jit(solution)/shard_map/all_gather | solution.py:42
  39.4 0.5 fusion.5
  39.9 0.4 copy.45
  40.3 0.3 reshape.30
  40.6 7.2 %all_to_all.45 = bf16[4,2,4608]{2,1,0:T(2,128)(2,1)S(1)} all-to-all(bf16[4,2,4608]{2,1,0:T(2,128)(2,1)S(1)} %reshape.30), channel_id=1, replica_groups=mesh['pr'=4,'pc'=8] {'pr'}, dimensions={0} | all-to-all | bytes 147456 | tf_op jit(solution)/shard_map/all_to_all | solution.py:47
  47.8 0.2 reshape.31
  48.1 0.3 copy.46
  48.4 0.4 reshape.21
  48.8 0.1 bitcast_reduce_fusion
  48.9 0.3 multiply_reduce_fusion
  49.2 0.3 copy.47
  49.5 0.0 copy-start.3
  49.5 0.3 reshape.19
  49.8 0.4 copy-done.3
  50.2 0.0 copy-start.2
  50.2 0.1 multiply_convert_fusion
  50.3 0.6 %copy-done.2 = bf16[128,128]{1,0:T(8,128)(2,1)S(1)} copy-done((bf16[128,128]{1,0:T(8,128)(2,1)S(1)}, bf16[128,128]{1,0:T(8,128)(2,1)}, u32[]{:S(2)}) %copy-start.2) | copy-done | bytes 32792
  50.9 0.0 copy-start.4
  50.9 0.2 fusion.10
  51.1 0.6 %copy-done.4 = bf16[128,128]{1,0:T(8,128)(2,1)S(1)} copy-done((bf16[128,128]{1,0:T(8,128)(2,1)S(1)}, bf16[128,128]{1,0:T(8,128)(2,1)}, u32[]{:S(2)}) %copy-start.4) | copy-done | bytes 32792
  51.7 0.8 %fusion.6 = bf16[24,12,128]{2,0,1:T(8,128)(2,1)} fusion(f32[24,12,128]{2,0,1:T(8,128)S(1)} %fusion.10, bf16[24,12,128]{2,0,1:T(8,128)(2,1)S(1)} %copy-done, bf16[128,128]{1,0:T(8,128)(2,1)S(1)} %copy-done.4), kind=kOutput, calls=%fused_computation.8 | convolution fusion | flops 9621504 | bytes 327680 | tf_op jit(solution)/shard_map/ijc,cd->ijd/dot_general | solution.py:26
  (2 shorter events, 0.0 us)
Async XLA Ops:
  0.0 0.9 %copy-start = (bf16[24,12,128]{2,0,1:T(8,128)(2,1)S(1)}, bf16[24,12,128]{2,0,1:T(8,128)(2,1)}, u32[]{:S(2)}) copy-start(bf16[24,12,128]{2,0,1:T(8,128)(2,1)} %param.6) | copy-start | bytes 221188
  3.4 5.3 %copy-start.1 = (bf16[128,128]{1,0:T(8,128)(2,1)S(1)}, bf16[128,128]{1,0:T(8,128)(2,1)}, u32[]{:S(2)}) copy-start(bf16[128,128]{1,0:T(8,128)(2,1)} %param.7) | copy-start | bytes 98308
  3.4 10.2 %all-to-all-start = ((bf16[4,2,4608]{2,1,0:T(2,128)(2,1)}), bf16[4,2,4608]{2,1,0:T(2,128)(2,1)S(1)}, u32[]{:S(2)}, u32[]{:S(2)}) async-start(bf16[4,2,4608]{2,1,0:T(2,128)(2,1)} %reshape.28), calls=%async_computation | async-start | bytes 147456 | tf_op jit(solution)/shard_map/all_to_all | solution.py:38
  13.6 8.1 %all-to-all-start.1 = ((bf16[4,2,4608]{2,1,0:T(2,128)(2,1)}), bf16[4,2,4608]{2,1,0:T(2,128)(2,1)S(1)}, u32[]{:S(2)}, u32[]{:S(2)}) async-start(bf16[4,2,4608]{2,1,0:T(2,128)(2,1)} %reshape.26), calls=%async_computation.1 | async-start | bytes 147456 | tf_op jit(solution)/shard_map/all_to_all | solution.py:37
  49.5 0.7 %copy-start.3 = (f32[128]{0:T(128)S(1)}, f32[128]{0:T(128)}, u32[]{:S(2)}) copy-start(f32[128]{0:T(128)} %param.9) | copy-start | bytes 1540
  50.2 0.8 %copy-start.2 = (bf16[128,128]{1,0:T(8,128)(2,1)S(1)}, bf16[128,128]{1,0:T(8,128)(2,1)}, u32[]{:S(2)}) copy-start(bf16[128,128]{1,0:T(8,128)(2,1)} %param.10) | copy-start | bytes 98308
  50.9 0.8 %copy-start.4 = (bf16[128,128]{1,0:T(8,128)(2,1)S(1)}, bf16[128,128]{1,0:T(8,128)(2,1)}, u32[]{:S(2)}) copy-start(bf16[128,128]{1,0:T(8,128)(2,1)} %param.11) | copy-start | bytes 98308
where the time goes:
time: 53.2 us; the launch traced here: 52.5 us
  blocking collectives  23.7 us (45%)
  local copies, waits for them, and re-layouts  10.1 us (19%)
  starting transfers between devices  8.61 us (16%)
  waiting for transfers between devices  6.78 us (13%)
  matrix products  2.61 us (5%)
  other arithmetic  0.54 us (1%)
    all_gather x1, blocking collectives, body(): lax.all_gather(left_lines, 'pc', axis=1, tiled=True)  16.5 us
    all_to_all x1, blocking collectives, body(): mixed = lax.all_to_all(strip, 'pr', split_axis=0, concat_axis=2, tiled=True)  7.24 us
    unnamed x16, local copies, waits for them, and re-layouts  6.51 us
    all_to_all x1, starting transfers between devices, body(): lax.all_to_all(right, 'pr', split_axis=2, concat_axis=0, tiled=True)  5.32 us
    all_to_all x1, waiting for transfers between devices, body(): lax.all_to_all(left, 'pr', split_axis=2, concat_axis=0, tiled=True)  3.68 us
    all_to_all x1, starting transfers between devices, body(): lax.all_to_all(left, 'pr', split_axis=2, concat_axis=0, tiled=True)  3.29 us
    all_to_all x1, waiting for transfers between devices, body(): lax.all_to_all(right, 'pr', split_axis=2, concat_axis=0, tiled=True)  3.1 us
  transfers between devices with their start and end apart: 2, of which 2 were waited for; matrix products, arithmetic and copies ran while one was open for 5% of the time, Pallas kernels for 0%

commit v1 on v0

--- a/solution.py
+++ b/solution.py
@@ -37,12 +37,21 @@
         lax.all_to_all(left, "pr", split_axis=2, concat_axis=0, tiled=True),
         lax.all_to_all(right, "pr", split_axis=2, concat_axis=0, tiled=True),
     )
-    strip = jnp.einsum(
-        "kid,kjd->ijd",
-        lax.all_gather(left_lines, "pc", axis=1, tiled=True),
-        right_lines,
-        preferred_element_type=jnp.float32,
-    )
+    x = left_lines
+    ways, here, hop = (lax.axis_size("pc"), lax.axis_index("pc"), x.shape[1])
+    results = []
+    for far in range(ways):
+        arriving = (
+            lax.ppermute(x, "pc", [(d, (d + 1) % ways) for d in range(ways)])
+            if far + 1 < ways
+            else x
+        )
+        results.append(
+            jnp.einsum("kid,kjd->ijd", x, right_lines, preferred_element_type=jnp.float32)
+        )
+        x = arriving
+    line = jnp.concatenate(results[::-1], axis=0)
+    strip = jnp.roll(line, (here + 1) * results[0].shape[0], axis=0)
     strip = (strip * count ** (-0.5)).astype(jnp.bfloat16)
     mixed = lax.all_to_all(strip, "pr", split_axis=0, concat_axis=2, tiled=True)
     return close_update(mixed, ready, mid_gain, out_weight, out_gate)

time: 53.2 us -> 77.9 us (1.46)
  waiting for transfers between devices: 6.78 us -> 43.4 us
  blocking collectives: 23.7 us -> 8.8 us
  local copies, waits for them, and re-layouts: 10.1 us -> 11.8 us
  matrix products: 2.61 us -> 3.5 us
    ppermute x0 -> x7, waiting for transfers between devices: none -> 36.8 us  [body(): lax.ppermute(x, 'pc', [(d, (d + 1) % ways) for d in range(ways)])]
    all_gather x1 -> x0, blocking collectives: 16.5 us -> none  [body(): lax.all_gather(left_lines, 'pc', axis=1, tiled=True)]
    all_to_all x1, starting transfers between devices: 5.32 us -> 3.29 us  [body(): lax.all_to_all(right, 'pr', split_axis=2, concat_axis=0, tiled=True)]
    all_to_all x1, starting transfers between devices: 3.29 us -> 5.32 us  [body(): lax.all_to_all(left, 'pr', split_axis=2, concat_axis=0, tiled=True)]
    all_to_all x1, blocking collectives: 7.24 us -> 8.8 us  [body(): mixed = lax.all_to_all(strip, 'pr', split_axis=0, concat_axis=2, tiled=True)]
    concatenate x0 -> x1, local copies, waits for them, and re-layouts: none -> 1.19 us  [body(): strip = jnp.roll(line, (here + 1) * results[0].shape[0], axis=0)]
    dot_general x1 -> x8, matrix products: 0.52 us -> 1.4 us  [body(): jnp.einsum('kid,kjd->ijd', x, right_lines, preferred_element_type=jnp.flo...]
  transfers between devices with their start and end apart: 2 -> 9, of which waited for: 2 -> 9; matrix products, arithmetic and copies ran while one was open for 5% -> 7% of each run, Pallas kernels for 0% -> 0%
where the time goes in v1:
time: 77.9 us; the launch traced here: 77.3 us
  waiting for transfers between devices  43.4 us (56%)
  local copies, waits for them, and re-layouts  11.8 us (15%)
  blocking collectives  8.8 us (11%)
  starting transfers between devices  8.68 us (11%)
  matrix products  3.5 us (4%)
    ppermute x7, waiting for transfers between devices, body(): lax.ppermute(x, 'pc', [(d, (d + 1) % ways) for d in range(ways)])  36.8 us
    all_to_all x1, blocking collectives, body(): mixed = lax.all_to_all(strip, 'pr', split_axis=0, concat_axis=2, tiled=True)  8.8 us
    unnamed x16, local copies, waits for them, and re-layouts  6.51 us
    all_to_all x1, starting transfers between devices, body(): lax.all_to_all(left, 'pr', split_axis=2, concat_axis=0, tiled=True)  5.32 us
    all_to_all x1, waiting for transfers between devices, body(): lax.all_to_all(right, 'pr', split_axis=2, concat_axis=0, tiled=True)  3.54 us
    all_to_all x1, starting transfers between devices, body(): lax.all_to_all(right, 'pr', split_axis=2, concat_axis=0, tiled=True)  3.29 us
    all_to_all x1, waiting for transfers between devices, body(): lax.all_to_all(left, 'pr', split_axis=2, concat_axis=0, tiled=True)  3.11 us
  transfers between devices with their start and end apart: 9, of which 9 were waited for; matrix products, arithmetic and copies ran while one was open for 7% of the time, Pallas kernels for 0%

profile of v1, /device:TPU:0, one launch (start us, length us, event | category | flops | bytes accessed | tf_op | source)
XLA Modules:
  0.0 77.3 jit_solution(11154329653775245327)
XLA Ops:
  0.0 0.9 %copy-done = bf16[24,12,128]{2,0,1:T(8,128)(2,1)S(1)} copy-done((bf16[24,12,128]{2,0,1:T(8,128)(2,1)S(1)}, bf16[24,12,128]{2,0,1:T(8,128)(2,1)}, u32[]{:S(2)}) %copy-start) | copy-done | bytes 73752
  0.9 0.9 %convolution_convert_fusion = bf16[24,12,128]{2,0,1:T(8,128)(2,1)S(1)} fusion(bf16[24,12,128]{2,0,1:T(8,128)(2,1)S(1)} %copy-done, bf16[128,128]{1,0:T(8,128)(2,1)} %param.7), kind=kOutput, calls=%fused_computation.6 | convolution fusion | flops 9474048 | bytes 180224 | tf_op jit(solution)/shard_map/ijc,cd->ijd/dot_general | solution.py:17
  1.8 0.4 copy.73
  2.3 1.1 %reshape.26 = bf16[4,2,4608]{2,1,0:T(2,128)(2,1)} reshape(bf16[128,12,24]{2,1,0:T(8,128)(2,1)S(1)} %bitcast.73) | data formatting | bytes 147456
  3.4 5.3 %all-to-all-start.1 = ((bf16[4,2,4608]{2,1,0:T(2,128)(2,1)}), bf16[4,2,4608]{2,1,0:T(2,128)(2,1)S(1)}, u32[]{:S(2)}, u32[]{:S(2)}) async-start(bf16[4,2,4608]{2,1,0:T(2,128)(2,1)} %reshape.26), calls=%async_computation.1 | async-start | bytes 147456 | tf_op jit(solution)/shard_map/all_to_all | solution.py:37
  8.7 0.2 convolution_convert_fusion.1
  8.9 0.4 copy.71
  9.4 1.1 %reshape.28 = bf16[4,2,4608]{2,1,0:T(2,128)(2,1)} reshape(bf16[128,12,24]{2,1,0:T(8,128)(2,1)S(1)} %bitcast.74) | data formatting | bytes 147456
  10.5 3.1 %all-to-all-done.1 = bf16[4,2,4608]{2,1,0:T(2,128)(2,1)S(1)} async-done(((bf16[4,2,4608]{2,1,0:T(2,128)(2,1)}), bf16[4,2,4608]{2,1,0:T(2,128)(2,1)S(1)}, u32[]{:S(2)}, u32[]{:S(2)}) %all-to-all-start.1) | async-done | bytes 73760 | tf_op jit(solution)/shard_map/all_to_all | solution.py:37
  13.6 3.3 %all-to-all-start = ((bf16[4,2,4608]{2,1,0:T(2,128)(2,1)}), bf16[4,2,4608]{2,1,0:T(2,128)(2,1)S(1)}, u32[]{:S(2)}, u32[]{:S(2)}) async-start(bf16[4,2,4608]{2,1,0:T(2,128)(2,1)} %reshape.28), calls=%async_computation | async-start | bytes 147456 | tf_op jit(solution)/shard_map/all_to_all | solution.py:38
  16.9 0.6 reshape.27
  17.5 0.3 copy.124
  17.8 0.2 all_to_all.40
  18.1 0.1 collective-permute-start
  18.2 3.5 %all-to-all-done = bf16[4,2,4608]{2,1,0:T(2,128)(2,1)S(1)} async-done(((bf16[4,2,4608]{2,1,0:T(2,128)(2,1)}), bf16[4,2,4608]{2,1,0:T(2,128)(2,1)S(1)}, u32[]{:S(2)}, u32[]{:S(2)}) %all-to-all-start) | async-done | bytes 73760 | tf_op jit(solution)/shard_map/all_to_all | solution.py:38
  21.7 0.6 reshape.29
  22.3 0.3 copy.125
  22.7 0.2 all_to_all.36
  22.9 0.2 fusion.5
  23.1 0.1 copy.126
  23.1 1.2 %collective-permute-done = bf16[96,12,32]{0,1,2:T(8,128)(2,1)S(1)} collective-permute-done((bf16[96,12,32]{0,1,2:T(8,128)(2,1)S(1)}, bf16[96,12,32]{0,1,2:T(8,128)(2,1)S(1)}, u32[]{:S(2)}, u32[]{:S(2)}) %collective-permute-start) | collective-permute-done | bytes 73760 | tf_op jit(solution)/shard_map/ppermute | solution.py:45
  24.4 0.0 collective-permute-start.1
  24.4 0.2 fusion.7
  24.6 0.1 copy.127
  24.6 5.9 %collective-permute-done.1 = bf16[96,12,32]{0,1,2:T(8,128)(2,1)S(1)} collective-permute-done((bf16[96,12,32]{0,1,2:T(8,128)(2,1)S(1)}, bf16[96,12,32]{0,1,2:T(8,128)(2,1)S(1)}, u32[]{:S(2)}, u32[]{:S(2)}) %collective-permute-start.1) | collective-permute-done | bytes 73760 | tf_op jit(solution)/shard_map/ppermute | solution.py:45
  30.6 0.0 collective-permute-start.2
  30.6 0.2 fusion.9
  30.7 0.1 copy.128
  30.8 5.9 %collective-permute-done.2 = bf16[96,12,32]{0,1,2:T(8,128)(2,1)S(1)} collective-permute-done((bf16[96,12,32]{0,1,2:T(8,128)(2,1)S(1)}, bf16[96,12,32]{0,1,2:T(8,128)(2,1)S(1)}, u32[]{:S(2)}, u32[]{:S(2)}) %collective-permute-start.2) | collective-permute-done | bytes 73760 | tf_op jit(solution)/shard_map/ppermute | solution.py:45
  36.8 0.0 collective-permute-start.3
  36.8 0.2 fusion.11
  36.9 0.1 copy.129
  37.0 5.9 %collective-permute-done.3 = bf16[96,12,32]{0,1,2:T(8,128)(2,1)S(1)} collective-permute-done((bf16[96,12,32]{0,1,2:T(8,128)(2,1)S(1)}, bf16[96,12,32]{0,1,2:T(8,128)(2,1)S(1)}, u32[]{:S(2)}, u32[]{:S(2)}) %collective-permute-start.3) | collective-permute-done | bytes 73760 | tf_op jit(solution)/shard_map/ppermute | solution.py:45
  43.0 0.2 fusion.13
  43.1 0.1 copy.130
  43.2 5.9 %collective-permute-done.4 = bf16[96,12,32]{0,1,2:T(8,128)(2,1)S(1)} collective-permute-done((bf16[96,12,32]{0,1,2:T(8,128)(2,1)S(1)}, bf16[96,12,32]{0,1,2:T(8,128)(2,1)S(1)}, u32[]{:S(2)}, u32[]{:S(2)}) %collective-permute-start.4) | collective-permute-done | bytes 73760 | tf_op jit(solution)/shard_map/ppermute | solution.py:45
  49.1 0.2 fusion.15
  49.3 0.1 copy.131
  49.4 5.9 %collective-permute-done.5 = bf16[96,12,32]{0,1,2:T(8,128)(2,1)S(1)} collective-permute-done((bf16[96,12,32]{0,1,2:T(8,128)(2,1)S(1)}, bf16[96,12,32]{0,1,2:T(8,128)(2,1)S(1)}, u32[]{:S(2)}, u32[]{:S(2)}) %collective-permute-start.5) | collective-permute-done | bytes 73760 | tf_op jit(solution)/shard_map/ppermute | solution.py:45
  55.3 0.0 collective-permute-start.6
  55.3 0.2 fusion.17
  55.5 0.1 copy.132
  55.6 5.9 %collective-permute-done.6 = bf16[96,12,32]{0,1,2:T(8,128)(2,1)S(1)} collective-permute-done((bf16[96,12,32]{0,1,2:T(8,128)(2,1)S(1)}, bf16[96,12,32]{0,1,2:T(8,128)(2,1)S(1)}, u32[]{:S(2)}, u32[]{:S(2)}) %collective-permute-start.6) | collective-permute-done | bytes 73760 | tf_op jit(solution)/shard_map/ppermute | solution.py:45
  61.5 0.2 fusion.19
  61.7 0.1 copy.133
  61.8 1.2 %concatenate.6 = f32[192,12,32]{0,2,1:T(8,128)S(1)} concatenate(f32[12,12,32]{0,2,1:T(8,128)S(1)} %bitcast.89, f32[12,12,32]{0,2,1:T(8,128)S(1)} %bitcast.87, f32[12,12,32]{0,2,1:T(8,128)S(1)} %bitcast.85, f32[12,12,32]{0,2,1:T(8,128)S(1)} %bitcast.83, f32[12,12,32]{0,2,1:T(8,128)S(1)} %bitcast.81, f32[12,12,32]{0,2,1:T(8,128)S(1)} %bitcast.79, f32[12,12,32]{0,2,1:T(8,128)S(1)} %bitcast.77, ...), dimensions={0} | concatenate | bytes 589824 | tf_op jit(solution)/shard_map/jit(_roll_dynamic)/concatenate | solution.py:54
  63.0 0.1 multiply_convert_fusion
  63.1 0.3 copy.93
  63.5 0.3 reshape.30
  63.8 8.8 %all_to_all.45 = bf16[4,2,4608]{2,1,0:T(2,128)(2,1)S(1)} all-to-all(bf16[4,2,4608]{2,1,0:T(2,128)(2,1)S(1)} %reshape.30), channel_id=1, replica_groups=mesh['pr'=4,'pc'=8] {'pr'}, dimensions={0} | all-to-all | bytes 147456 | tf_op jit(solution)/shard_map/all_to_all | solution.py:56
  72.6 0.2 reshape.31
  72.8 0.3 copy.94
  73.1 0.4 reshape.21
  73.5 0.1 bitcast_reduce_fusion
  73.7 0.3 multiply_reduce_fusion
  73.9 0.3 copy.95
  74.3 0.0 copy-start.3
  74.3 0.3 reshape.19
  74.6 0.4 copy-done.3
  74.9 0.1 multiply_convert_fusion.1
  75.1 0.6 copy-done.2
  75.7 0.2 fusion.22
  75.8 0.6 copy-done.4
  76.4 0.8 %fusion.4 = bf16[24,12,128]{2,0,1:T(8,128)(2,1)} fusion(f32[24,12,128]{2,0,1:T(8,128)S(1)} %fusion.22, bf16[24,12,128]{2,0,1:T(8,128)(2,1)S(1)} %copy-done, bf16[128,128]{1,0:T(8,128)(2,1)S(1)} %copy-done.4), kind=kOutput, calls=%fused_computation.5 | convolution fusion | flops 9621504 | bytes 327680 | tf_op jit(solution)/shard_map/ijc,cd->ijd/dot_general | solution.py:26
  (10 shorter events, 0.1 us)
Async XLA Ops:
  0.0 0.9 %copy-start = (bf16[24,12,128]{2,0,1:T(8,128)(2,1)S(1)}, bf16[24,12,128]{2,0,1:T(8,128)(2,1)}, u32[]{:S(2)}) copy-start(bf16[24,12,128]{2,0,1:T(8,128)(2,1)} %param.6) | copy-start | bytes 221188
  3.4 5.3 %copy-start.1 = (bf16[128,128]{1,0:T(8,128)(2,1)S(1)}, bf16[128,128]{1,0:T(8,128)(2,1)}, u32[]{:S(2)}) copy-start(bf16[128,128]{1,0:T(8,128)(2,1)} %param.8) | copy-start | bytes 98308
  3.4 10.2 %all-to-all-start.1 = ((bf16[4,2,4608]{2,1,0:T(2,128)(2,1)}), bf16[4,2,4608]{2,1,0:T(2,128)(2,1)S(1)}, u32[]{:S(2)}, u32[]{:S(2)}) async-start(bf16[4,2,4608]{2,1,0:T(2,128)(2,1)} %reshape.26), calls=%async_computation.1 | async-start | bytes 147456 | tf_op jit(solution)/shard_map/all_to_all | solution.py:37
  13.6 8.1 %all-to-all-start = ((bf16[4,2,4608]{2,1,0:T(2,128)(2,1)}), bf16[4,2,4608]{2,1,0:T(2,128)(2,1)S(1)}, u32[]{:S(2)}, u32[]{:S(2)}) async-start(bf16[4,2,4608]{2,1,0:T(2,128)(2,1)} %reshape.28), calls=%async_computation | async-start | bytes 147456 | tf_op jit(solution)/shard_map/all_to_all | solution.py:38
  18.1 6.2 %collective-permute-start = (bf16[96,12,32]{0,1,2:T(8,128)(2,1)S(1)}, bf16[96,12,32]{0,1,2:T(8,128)(2,1)S(1)}, u32[]{:S(2)}, u32[]{:S(2)}) collective-permute-start(bf16[96,12,32]{0,1,2:T(8,128)(2,1)S(1)} %copy.75), channel_id=1, source_target_pairs={{0,1},{1,2},{2,3},{3,4},{4,5},{5,6},{6,7},{7,0},{8,9},{9,10},{10,1... | collective-permute-start | bytes 221192 | tf_op jit(solution)/shard_map/ppermute | solution.py:45
  24.4 6.2 %collective-permute-start.1 = (bf16[96,12,32]{0,1,2:T(8,128)(2,1)S(1)}, bf16[96,12,32]{0,1,2:T(8,128)(2,1)S(1)}, u32[]{:S(2)}, u32[]{:S(2)}) collective-permute-start(bf16[96,12,32]{0,1,2:T(8,128)(2,1)S(1)} %collective-permute-done), channel_id=1, source_target_pairs={{0,1},{1,2},{2,3},{3,4},{4,5},{5,6},{6,7},{7,0},{8,9},{9,10},{10,1... | collective-permute-start | bytes 221192 | tf_op jit(solution)/shard_map/ppermute | solution.py:45
  30.6 6.2 %collective-permute-start.2 = (bf16[96,12,32]{0,1,2:T(8,128)(2,1)S(1)}, bf16[96,12,32]{0,1,2:T(8,128)(2,1)S(1)}, u32[]{:S(2)}, u32[]{:S(2)}) collective-permute-start(bf16[96,12,32]{0,1,2:T(8,128)(2,1)S(1)} %collective-permute-done.1), channel_id=1, source_target_pairs={{0,1},{1,2},{2,3},{3,4},{4,5},{5,6},{6,7},{7,0},{8,9},{9,10},{10,1... | collective-permute-start | bytes 221192 | tf_op jit(solution)/shard_map/ppermute | solution.py:45
  36.8 6.2 %collective-permute-start.3 = (bf16[96,12,32]{0,1,2:T(8,128)(2,1)S(1)}, bf16[96,12,32]{0,1,2:T(8,128)(2,1)S(1)}, u32[]{:S(2)}, u32[]{:S(2)}) collective-permute-start(bf16[96,12,32]{0,1,2:T(8,128)(2,1)S(1)} %collective-permute-done.2), channel_id=1, source_target_pairs={{0,1},{1,2},{2,3},{3,4},{4,5},{5,6},{6,7},{7,0},{8,9},{9,10},{10,1... | collective-permute-start | bytes 221192 | tf_op jit(solution)/shard_map/ppermute | solution.py:45
  42.9 6.2 %collective-permute-start.4 = (bf16[96,12,32]{0,1,2:T(8,128)(2,1)S(1)}, bf16[96,12,32]{0,1,2:T(8,128)(2,1)S(1)}, u32[]{:S(2)}, u32[]{:S(2)}) collective-permute-start(bf16[96,12,32]{0,1,2:T(8,128)(2,1)S(1)} %collective-permute-done.3), channel_id=1, source_target_pairs={{0,1},{1,2},{2,3},{3,4},{4,5},{5,6},{6,7},{7,0},{8,9},{9,10},{10,1... | collective-permute-start | bytes 221192 | tf_op jit(solution)/shard_map/ppermute | solution.py:45
  49.1 6.2 %collective-permute-start.5 = (bf16[96,12,32]{0,1,2:T(8,128)(2,1)S(1)}, bf16[96,12,32]{0,1,2:T(8,128)(2,1)S(1)}, u32[]{:S(2)}, u32[]{:S(2)}) collective-permute-start(bf16[96,12,32]{0,1,2:T(8,128)(2,1)S(1)} %collective-permute-done.4), channel_id=1, source_target_pairs={{0,1},{1,2},{2,3},{3,4},{4,5},{5,6},{6,7},{7,0},{8,9},{9,10},{10,1... | collective-permute-start | bytes 221192 | tf_op jit(solution)/shard_map/ppermute | solution.py:45
  55.3 6.2 %collective-permute-start.6 = (bf16[96,12,32]{0,1,2:T(8,128)(2,1)S(1)}, bf16[96,12,32]{0,1,2:T(8,128)(2,1)S(1)}, u32[]{:S(2)}, u32[]{:S(2)}) collective-permute-start(bf16[96,12,32]{0,1,2:T(8,128)(2,1)S(1)} %collective-permute-done.5), channel_id=1, source_target_pairs={{0,1},{1,2},{2,3},{3,4},{4,5},{5,6},{6,7},{7,0},{8,9},{9,10},{10,1... | collective-permute-start | bytes 221192 | tf_op jit(solution)/shard_map/ppermute | solution.py:45
  74.3 0.7 copy-start.3
  74.9 0.8 copy-start.2
  75.7 0.8 copy-start.4
